TPU v7x, 128 devices: a whole 4x4x4 slice. The times are simulated.
128 devices in a mesh: dom: 32 (over x, y, core), shift: 4 (over z).
Axes of the slice: x: 4, y: 4, z: 4, core: 2. Of those that a mesh axis runs over, the one named last changes fastest.
Arguments:
- sources: float32 [32, 128, 16, 128], P('shift', 'dom'), may hold values from -6 to 6
- kappa: float32 [128, 16, 128], P('dom'), may hold values from 0 to 2
- mass: float32 [128, 16, 128], P('dom'), may hold values from 0.25 to 4
- shift_table: float32 [64], replicated, may hold values from 0.5 to 4
- shift_ids: int32 [16], P('shift'), may hold values from 0 to 63
- sketch: bfloat16 [1024, 128, 16, 128], P(None, 'dom'), may hold values from -0.1875 to 0.1875
Outputs:
- solution: float32 [16, 32, 128, 16, 128], P('shift', None, 'dom')
- residual: float32 [16, 32, 128, 16, 128], P('shift', None, 'dom')
Inputs may be any that keep to these rules, and one draw needn't show every extreme that they name: `shift_ids`: index into shift_table.
All inputs are finite; a program needn't handle non-finite values.
Results may differ from a plain program's by a relative error of at most 0.0026.
Values sent between devices are 32-bit elements; how exact they have to be, the bound alone decides.
No kernel may reach another device: no remote copies, remote signals or barrier semaphores. Data moves between devices by JAX's collectives and lax.ppermute only.
A program may use at most 128 MiB of HBM per device.

v0:
```python
import functools

import jax
import jax.numpy as jnp
from jax import lax
from jax.experimental import pallas as pl
from jax.experimental.pallas import tpu as pltpu
from jax.sharding import PartitionSpec as P


BOTH = ("dom", "shift")
FIELDS = 10
LEVEL = (0, 1, 1, 2, 2, 2, 3, 3, 3, 3)
POWER = (0, 0, 1, 0, 1, 2, 0, 1, 2, 3)
SIGN = (1.0, -1.0, 1.0, 1.0, -1.0, 1.0, -1.0, 1.0, -1.0, 1.0)
PITCH = 12
BLOCKS = 4
CHUNKS = 4
VMEM = pl.BlockSpec(memory_space=pltpu.VMEM)
SMEM = pl.BlockSpec(memory_space=pltpu.SMEM)


def around(field):
    inner = field[1:-1]
    rows = lax.broadcasted_iota(jnp.int32, inner.shape, 1)
    lanes = lax.broadcasted_iota(jnp.int32, inner.shape, 2)
    ny, nz = inner.shape[1], inner.shape[2]
    total = field[2:] + field[:-2]
    total = total + jnp.where(rows == 0, 0.0, pltpu.roll(inner, 1, 1))
    total = total + jnp.where(rows == ny - 1, 0.0, pltpu.roll(inner, ny - 1, 1))
    total = total + jnp.where(lanes == 0, 0.0, pltpu.roll(inner, 1, 2))
    return total + jnp.where(lanes == nz - 1, 0.0, pltpu.roll(inner, nz - 1, 2))


def masked(field, count, low, high):
    return jnp.concatenate([field[:count] * low, field[count:-count], field[-count:] * high], axis=0)


def ten_fields(w, kappa, q, low, high):
    def p(field, planes):
        cut = (kappa.shape[0] - planes) // 2
        return kappa[cut : cut + planes] * field[1:-1] + around(field)

    slab = w.shape[0] - 6
    e10 = masked(p(w, slab + 4), 2, low, high)
    e01 = q[1:-1] * w[1:-1]
    e20 = masked(p(e10, slab + 2), 1, low, high)
    e11 = masked(p(e01, slab + 2) + q[2:-2] * e10[1:-1], 1, low, high)
    e02 = q[2:-2] * e01[1:-1]
    q3 = q[3:-3]
    e30 = p(e20, slab)
    e21 = p(e11, slab) + q3 * e20[1:-1]
    e12 = p(e02, slab) + q3 * e11[1:-1]
    e03 = q3 * e02[1:-1]
    return (w[3:-3], e10[2:-2], e01[2:-2], e20[1:-1], e11[1:-1], e02[1:-1], e30, e21, e12, e03)


def edges_kernel(kappa, mass, sources, top, bottom, own, sem):
    slab = kappa.shape[0]
    copies = []
    for out, cut in ((top, pl.ds(slab - 3, 3)), (bottom, pl.ds(0, 3)), (own, pl.ds(0, slab))):
        for source, target in (
            (kappa.at[cut], out.at[0]),
            (mass.at[cut], out.at[1]),
            (sources.at[:, cut], out.at[pl.ds(2, sources.shape[0])]),
        ):
            copies.append(pltpu.make_async_copy(source, target, sem.at[len(copies)]))
    for copy in copies:
        copy.start()
    for copy in copies:
        copy.wait()


def sketch_kernel(edge, low, high, own, sketch, out, near, held, fld, right, acc0, acc1, cols, sem, kept):
    sources = own.shape[0] - 2
    slab, ny, nz = own.shape[1:]
    pairs, rows = held.shape[0], held.shape[1]
    chunks = sem.shape[0]
    run = pairs // chunks

    def fetch(c, k):
        return pltpu.make_async_copy(sketch.at[:, k], held.at[k], sem.at[c])

    for c in range(chunks):
        for k in range(run):
            fetch(c, c * run + k).start()

    low_on, high_on = edge[0], edge[1]
    wide_kappa = jnp.concatenate([low[0], own[0], high[0]], axis=0)
    q = jnp.concatenate([low[1], own[1], high[1]], axis=0) - 1.0
    pitch = fld.shape[0] // (FIELDS * sources)

    def one_source(s, carry):
        wide = jnp.concatenate([low[s + 2], own[s + 2], high[s + 2]], axis=0)
        for f, field in enumerate(ten_fields(wide, wide_kappa, q, low_on, high_on)):
            start = pl.multiple_of((f * sources + s) * pitch, 8)
            fld[pl.ds(start, slab * ny), :] = field.reshape(slab * ny, nz)
        return carry

    lax.fori_loop(0, sources, one_source, 0)
    keep = pltpu.make_async_copy(fld, near, kept)
    keep.start()
    columns = FIELDS * sources
    for k in range(pairs):
        for parity in range(2):
            line = fld[pl.ds(2 * k + parity, columns, stride=pitch), :]
            right[pl.ds(parity * 128, columns), k * nz : (k + 1) * nz] = line.astype(jnp.bfloat16)

    block = 2 * rows // BLOCKS
    for c in range(chunks):
        for k in range(run):
            fetch(c, c * run + k).wait()
        weights = right[:, c * run * nz : (c + 1) * run * nz]
        for b in range(BLOCKS):
            at = slice(b * block, (b + 1) * block)
            left = jnp.concatenate(
                [held[c * run + k, b * block // 2 : (b + 1) * block // 2].reshape(block, nz) for k in range(run)],
                axis=1,
            )
            both = lax.dot_general(left, weights, (((1,), (1,)), ((), ())), preferred_element_type=jnp.float32)
            if c > 0:
                both = both + jnp.concatenate([acc0[at, :], acc1[at, :]], axis=1)
            acc0[at, :] = both[:, :128]
            acc1[at, :] = both[:, 128:]

    strips = rows // 128
    per_piece = strips * sources // out.shape[0]
    for t in range(strips):
        line = acc0[pl.ds(t * 256, 128, stride=2), :] + acc1[pl.ds(t * 256 + 1, 128, stride=2), :]
        cols[t] = line.T
    for t in range(strips):
        for s in range(sources):
            piece = s * (strips // per_piece) + t // per_piece
            place = FIELDS * (t % per_piece)
            out[piece, place : place + FIELDS, :] = cols.at[t][pl.ds(s, FIELDS, stride=sources), :]
    for piece in range(out.shape[0]):
        used = FIELDS * per_piece
        out[piece, used:, :] = jnp.zeros((out.shape[1] - used, 128), jnp.float32)
    keep.wait()


def gram_kernel(pieces, out):
    rows = pieces[0]
    for peer in range(1, pieces.shape[0]):
        rows = rows + pieces[peer]
    gram = lax.dot_general(
        rows, rows, (((1,), (1,)), ((), ())), preferred_element_type=jnp.float32, precision=lax.Precision.HIGHEST
    )
    gram = gram[:FIELDS, :FIELDS] + gram[FIELDS : 2 * FIELDS, FIELDS : 2 * FIELDS]
    wide = jnp.concatenate([gram, jnp.zeros((FIELDS, 128 - FIELDS), jnp.float32)], axis=1)
    line = wide[0:1]
    for f in range(1, FIELDS):
        line = line + pltpu.roll(wide[f : f + 1], PITCH * f, 1)
    out[...] = jnp.broadcast_to(line[None], out.shape)


def load_kernel(_, low, high, after, before, to_after, to_before, sem):
    ends = low.shape[0] - 6
    kept = to_after.shape[0] - 2 * ends
    copies = []
    for out, slab, start in ((to_after, after, 0), (to_before, before, kept)):
        for source, target in (
            (low.at[pl.ds(6, ends)], out.at[pl.ds(0, ends)]),
            (high.at[pl.ds(6, ends)], out.at[pl.ds(ends, ends)]),
            (slab.at[pl.ds(start, kept)], out.at[pl.ds(2 * ends, kept)]),
        ):
            copies.append(pltpu.make_async_copy(source, target, sem.at[len(copies)]))
    for copy in copies:
        copy.start()
    for copy in copies:
        copy.wait()


def far_kernel(parts, outside, edge, kappa, mass, low, high, *refs):
    planes = list(refs[: len(refs) - 1 - len(outside) - bool(outside)])
    out, *held = refs[len(planes) :]
    if outside:
        *held, sem = held
        copies = [pltpu.make_async_copy(planes[n], ref, sem.at[i]) for i, (n, ref) in enumerate(zip(outside, held))]

        @pl.when(pl.program_id(0) == 0)
        def _():
            for copy in copies:
                copy.start()
            for copy in copies:
                copy.wait()

        for n, ref in zip(outside, held):
            planes[n] = ref
    low_on, high_on = edge[0], edge[1]
    wide_kappa = jnp.concatenate([low[0], kappa[...], high[0]], axis=0)
    q = jnp.concatenate([low[1], mass[...], high[1]], axis=0) - 1.0
    slab, ny, nz = kappa.shape
    here = out.shape[0]
    step = pl.program_id(0)
    base = 0
    for count, below, middle, above in parts:

        @pl.when((step >= base) & (step < base + count // here))
        def _(base=base, below=below, middle=middle, above=above):
            def one_source(i, carry):
                s = (step - base) * here + i

                def cut(place, size):
                    ref, first = place
                    return planes[ref][pl.ds(first + s * size, size)]

                wide = jnp.concatenate([cut(below, 3), cut(middle, slab), cut(above, 3)], axis=0)
                for f, field in enumerate(ten_fields(wide, wide_kappa, q, low_on, high_on)):
                    out[i, f] = field.reshape(slab * ny, nz)
                return carry

            lax.fori_loop(0, here, one_source, 0)

        base = base + count // here


def solve_small(gram):
    ridge = 0.001 * (gram[1][1] + gram[2][2] + gram[3][3]) / 3.0 + 1.0
    entry = [[gram[1 + i][1 + k] + (ridge if i == k else 0.0) for k in range(3)] for i in range(3)]
    h = [gram[1 + i][0] for i in range(3)]
    l00 = jnp.sqrt(entry[0][0])
    l10 = entry[1][0] / l00
    l20 = entry[2][0] / l00
    l11 = jnp.sqrt(entry[1][1] - l10 * l10)
    l21 = (entry[2][1] - l20 * l10) / l11
    l22 = jnp.sqrt(entry[2][2] - l20 * l20 - l21 * l21)
    f0 = h[0] / l00
    f1 = (h[1] - l10 * f0) / l11
    f2 = (h[2] - l20 * f0 - l21 * f1) / l22
    c2 = f2 / l22
    c1 = (f1 - l21 * c2) / l11
    c0 = (f0 - l10 * c1 - l20 * c2) / l00
    return c0, c1, c2


def relative_group(step, per):
    place = step // per
    return jnp.where(place == 2, 3, jnp.where(place == 3, 2, place))


def final_kernel(
    group, table, ids, grams, near_hbm, beside_hbm, beyond_hbm, sol, res, near, far, turned, weights, scalars, sem, arrived
):
    groups = 4
    per_group = grams.shape[0] // (groups * groups)
    shifts = ids.shape[0]
    step = pl.program_id(0)
    here = sol.shape[1]
    near_steps = per_group // here
    beside_steps = beside_hbm.shape[0] // here

    def fetch(n):
        if n == 0:
            return pltpu.make_async_copy(near_hbm, near, arrived.at[0])
        source, first = (beside_hbm, 0) if n <= beside_steps else (beyond_hbm, beside_steps)
        taken = source.at[pl.ds((n - 1 - first) * here, here)]
        return pltpu.make_async_copy(taken, far.at[pl.ds((n - 1) * here, here)], arrived.at[n])

    copies = 1 + far.shape[0] // here

    @pl.when(step == 0)
    def _():
        for n in range(copies):
            fetch(n).start()
        parts = grams.shape[0] // (groups * per_group)
        flat = grams.reshape(grams.shape[0], 128)
        lines = []
        for g in range(groups):
            line = None
            for part in range(parts):
                one = flat[pl.ds(part * groups + g, per_group, stride=parts * groups), :]
                line = one if line is None else line + one
            lines.append(line)
        gram = jnp.concatenate(lines, axis=0)
        turned[...] = jnp.concatenate([gram, jnp.zeros((128 - gram.shape[0], 128), jnp.float32)], axis=0).T
        shape = (8, 128)
        line = lax.broadcasted_iota(jnp.int32, shape, 0)
        sigma = jnp.zeros(shape, jnp.float32)
        for j in range(shifts):
            sigma = jnp.where(line == j, table[ids[j]], sigma)
        terms = {}
        for f in range(FIELDS):
            for e in range(f, FIELDS):
                place = PITCH * f + e
                value = jnp.broadcast_to(turned[place : place + 1, :], shape)
                sign = SIGN[f] * SIGN[e] * (2.0 if LEVEL[f] == LEVEL[e] and f != e else 1.0)
                value = value if sign == 1.0 else value * sign
                key = (LEVEL[f], LEVEL[e], POWER[f] + POWER[e])
                terms[key] = terms[key] + value if key in terms else value
        inner = [[None] * 4 for _ in range(4)]
        for a in range(4):
            for b in range(a, 4):
                value = terms[(a, b, a + b)]
                for power in range(a + b - 1, -1, -1):
                    value = value * sigma + terms[(a, b, power)]
                value = value * (1.0 / 6.0 ** (a + b))
                inner[a][b] = inner[b][a] = value
        center = 6.0 + sigma
        mixed = [[6.0 * inner[i + 1][k] + center * inner[i][k] for k in range(4)] for i in range(3)]
        full = [[None] * 4 for _ in range(4)]
        for i in range(3):
            full[1 + i][0] = mixed[i][0]
            for k in range(3):
                full[1 + i][1 + k] = 6.0 * mixed[i][k + 1] + center * mixed[i][k]
        c0, c1, c2 = solve_small(full)
        values = (
            c0,
            c1 * (1.0 / 6.0),
            c2 * (1.0 / 36.0),
            1.0 - c0 * center,
            (6.0 * c0 + c1 * center) * (-1.0 / 6.0),
            (6.0 * c1 + c2 * center) * (-1.0 / 36.0),
            c2 * (-1.0 / 36.0),
        )
        for n, value in enumerate(values):
            weights[8 * n : 8 * (n + 1), :] = value
        copy = pltpu.make_async_copy(weights, scalars, sem)
        copy.start()
        copy.wait()

    ny = sol.shape[3]
    pitch = near.shape[0] // (FIELDS * per_group)
    steps_per_group = per_group // here
    ahead = relative_group(step, steps_per_group)
    first = lax.rem(group[0] + ahead, groups) * per_group + lax.rem(step, steps_per_group) * here

    def combine(read):
        for i in range(here):
            c = [[scalars[8 * n + j, first + i] for n in range(7)] for j in range(shifts)]
            for p in range(sol.shape[2]):
                w, e10, e01, e20, e11, e02, e30, e21, e12, e03 = (read(i, f, p * ny) for f in range(FIELDS))
                for j in range(shifts):
                    x = table[ids[j]]
                    c0, c1, c2, b0, b1, b2, b3 = c[j]
                    v1 = x * e01 - e10
                    v2 = x * (x * e02 - e11) + e20
                    v3 = x * (x * (x * e03 - e12) + e21) - e30
                    sol[j, i, p] = c0 * w + c1 * v1 + c2 * v2
                    res[j, i, p] = b0 * w + b1 * v1 + b2 * v2 + b3 * v3

    @pl.when(step < near_steps)
    def _():
        @pl.when(step == 0)
        def _():
            fetch(0).wait()

        def read(i, f, at):
            return near[pl.ds(pl.multiple_of((f * per_group + step * here + i) * pitch, 8) + at, ny), :]

        combine(read)

    @pl.when(step >= near_steps)
    def _():
        for n in range(1, copies):

            @pl.when(step == near_steps + n - 1)
            def _(n=n):
                fetch(n).wait()

        combine(lambda i, f, at: far[(step - near_steps) * here + i, f, at : at + ny, :])


def cost(us):
    return pl.CostEstimate(flops=int(us * 8e6), bytes_accessed=0, transcendentals=0)


def limit(mib):
    return pltpu.CompilerParams(vmem_limit_bytes=mib << 20)


def on_device(sources, kappa, mass, shift_table, shift_ids, sketch):
    f32 = jnp.float32
    dom, shift = lax.axis_size("dom"), lax.axis_size("shift")
    per_group, slab, ny, nz = sources.shape
    total = per_group * shift
    rows = sketch.shape[0]
    pairs = slab * ny // 2
    at = lax.axis_index("dom")
    edge = jnp.stack([at > 0, at < dom - 1]).astype(f32)
    group = lax.axis_index("shift").astype(jnp.int32)[None]

    HBM = pl.BlockSpec(memory_space=pltpu.HBM)

    def in_hbm(array):
        return pltpu.with_memory_space_constraint(array, pltpu.HBM)

    coeffs = (in_hbm(kappa), in_hbm(mass))
    ends = pltpu.VMEM((2 + per_group, 3, ny, nz), f32)
    top, bottom, own = pl.pallas_call(
        edges_kernel,
        in_specs=[HBM] * 3,
        out_specs=[VMEM] * 3,
        out_shape=[ends, ends, pltpu.VMEM((2 + per_group, slab, ny, nz), f32)],
        scratch_shapes=[pltpu.SemaphoreType.DMA((9,))],
        name="edges",
    )(*coeffs, in_hbm(sources))
    low = lax.ppermute(top, "dom", [(i, i + 1) for i in range(dom - 1)])
    high = lax.ppermute(bottom, "dom", [(i + 1, i) for i in range(dom - 1)])
    from_next = [(i, (i - 1) % shift) for i in range(shift)]
    from_last = [(i, (i + 1) % shift) for i in range(shift)]
    half = per_group // 2
    after = lax.ppermute(sources, "shift", from_next)
    before = lax.ppermute(sources, "shift", from_last)

    pitch = slab * ny + 8
    pieces, near = pl.pallas_call(
        sketch_kernel,
        in_specs=[SMEM] + [VMEM] * 3 + [HBM],
        out_specs=[VMEM, HBM],
        out_shape=[
            pltpu.VMEM((dom, 24, 128), f32),
            pltpu.HBM((FIELDS * per_group * pitch, nz), f32),
        ],
        scratch_shapes=[
            pltpu.VMEM((pairs, rows, 2, nz), jnp.bfloat16),
            pltpu.VMEM((FIELDS * per_group * pitch, nz), f32),
            pltpu.VMEM((256, pairs * nz), jnp.bfloat16),
            pltpu.VMEM((2 * rows, 128), f32),
            pltpu.VMEM((2 * rows, 128), f32),
            pltpu.VMEM((rows // 128, 128, 128), f32),
            pltpu.SemaphoreType.DMA((CHUNKS,)),
            pltpu.SemaphoreType.DMA,
        ],
        compiler_params=limit(36),
        cost_estimate=cost(12),
        name="sketch_fields",
    )(edge, low, high, own, in_hbm(sketch.reshape(rows, pairs, 2, nz)))
    arrived = lax.all_to_all(pieces, "dom", 0, 0, tiled=True)

    def flat(array):
        return array.reshape(-1, ny, nz)

    ends, skip = 3 * per_group, 3 * half
    load = pltpu.VMEM((2 * ends + half * slab, ny, nz), f32)
    load_after, load_before = pl.pallas_call(
        load_kernel,
        in_specs=[HBM] + [pl.BlockSpec(memory_space=pl.ANY)] * 2 + [HBM] * 2,
        out_specs=[VMEM] * 2,
        out_shape=[load, load],
        scratch_shapes=[pltpu.SemaphoreType.DMA((6,))],
        name="load",
    )(near, flat(low), flat(high), in_hbm(flat(after)), in_hbm(flat(before)))
    second_after = lax.ppermute(load_after, "shift", from_next)
    second_before = lax.ppermute(load_before, "shift", from_last)

    def third(array, start):
        return jnp.concatenate([array[start : start + skip], array[ends + start : ends + start + skip]])

    third_after = lax.ppermute(third(second_after, 0), "shift", from_next)
    third_before = lax.ppermute(third(second_before, skip), "shift", from_last)

    here = 4

    def far_fields(parts, outside, *planes):
        count = sum(part[0] for part in parts)
        shape = (count, FIELDS, slab * ny, nz)
        return pl.pallas_call(
            functools.partial(far_kernel, parts, outside),
            in_specs=[SMEM] + [VMEM] * 4 + [HBM if n in outside else VMEM for n in range(len(planes))],
            grid=(count // here,),
            out_specs=pl.BlockSpec((here, *shape[1:]), lambda i: (i, 0, 0, 0)),
            out_shape=pltpu.HBM(shape, f32),
            scratch_shapes=[pltpu.VMEM(planes[n].shape, f32) for n in outside]
            + [pltpu.SemaphoreType.DMA((len(outside),))] * bool(outside),
            compiler_params=limit(20),
            cost_estimate=cost(count * 0.3),
        )(edge, kappa, mass, low, high, *planes)

    lines = pl.pallas_call(
        gram_kernel,
        in_specs=[VMEM],
        out_specs=VMEM,
        out_shape=pltpu.VMEM((dom * shift, 1, 128), f32),
        cost_estimate=cost(2),
        name="gram",
    )(pltpu.with_memory_space_constraint(arrived, pltpu.VMEM))
    grams = lax.all_to_all(lines, BOTH, 0, 0, tiled=True)
    beside = far_fields(
        ((per_group, (0, 0), (1, 0), (0, ends)), (per_group, (2, 0), (3, 0), (2, ends))),
        (1, 3),
        second_after, in_hbm(flat(after)), second_before, in_hbm(flat(before)),
    )
    beyond = far_fields(
        ((half, (0, 0), (1, 2 * ends), (0, skip)), (half, (2, 0), (3, 2 * ends), (2, skip))),
        (),
        third_after, second_after, third_before, second_before,
    )

    here = per_group
    steps = total // here
    shifts = shift_ids.shape[0]
    per = per_group // here

    def place(i, group):
        return (0, lax.rem(group[0] + relative_group(i, per), shift) * per + lax.rem(i, per), 0, 0, 0)

    spec = pl.BlockSpec((shifts, here, slab, ny, nz), place)
    shape = jax.ShapeDtypeStruct((shifts, total, slab, ny, nz), f32)
    return pl.pallas_call(
        final_kernel,
        grid_spec=pltpu.PrefetchScalarGridSpec(
            num_scalar_prefetch=1,
            grid=(steps,),
            in_specs=[SMEM, SMEM, VMEM, HBM, HBM, HBM],
            out_specs=[spec, spec],
            scratch_shapes=[
                pltpu.VMEM(near.shape, f32),
                pltpu.VMEM((total - per_group, FIELDS, slab * ny, nz), f32),
                pltpu.VMEM((128, 128), f32),
                pltpu.VMEM((56, 128), f32),
                pltpu.SMEM((56, 128), f32),
                pltpu.SemaphoreType.DMA,
                pltpu.SemaphoreType.DMA((1 + (total - per_group) // here,)),
            ],
        ),
        out_shape=[shape, shape],
        compiler_params=limit(36),
        name="combine",
    )(group, shift_table, shift_ids, grams, in_hbm(near), in_hbm(beside), in_hbm(beyond))


def solution(mesh):
    placed = (
        P("shift", "dom", None, None),
        P("dom", None, None),
        P("dom", None, None),
        P(),
        P("shift"),
        P(None, "dom", None, None),
    )

    def body(*args):
        return tuple(on_device(*args))

    return jax.shard_map(
        body,
        mesh=mesh,
        in_specs=placed,
        out_specs=(P("shift", None, "dom", None, None), P("shift", None, "dom", None, None)),
        check_vma=False,
    )
```

profile of v0, /device:TPU:1, one launch (start us, length us, event | category | flops | bytes accessed | tf_op | source)
XLA Modules:
  0.0 79.1 jit_solution(9627556068155466668)
XLA Ops:
  0.6 2.5 %collective-permute-start.3 = (f32[8,4,16,128]{3,2,1,0:T(8,128)}, f32[8,4,16,128]{3,2,1,0:T(8,128)S(1)}, u32[]{:S(2)}, u32[]{:S(2)}) collective-permute-start(f32[8,4,16,128]{3,2,1,0:T(8,128)} %sources.1), channel_id=1, source_target_pairs={{0,1},{1,2},{2,3},{3,0},{4,5},{5,6},{6,7},{7,4},{8,9},{9,10},{10,1... | collective-permute-start | bytes 786440 | tf_op jit(solution)/shard_map/ppermute | solution.py:404
  3.2 2.2 %collective-permute-start.2 = (f32[8,4,16,128]{3,2,1,0:T(8,128)}, f32[8,4,16,128]{3,2,1,0:T(8,128)S(1)}, u32[]{:S(2)}, u32[]{:S(2)}) collective-permute-start(f32[8,4,16,128]{3,2,1,0:T(8,128)} %sources.1), channel_id=1, source_target_pairs={{0,3},{1,0},{2,1},{3,2},{4,7},{5,4},{6,5},{7,6},{8,11},{9,8},{10,9... | collective-permute-start | bytes 786440 | tf_op jit(solution)/shard_map/ppermute | solution.py:403
  5.4 1.3 %edges.1 = (f32[10,3,16,128]{3,2,1,0:T(8,128)S(1)}, f32[10,3,16,128]{3,2,1,0:T(8,128)S(1)}, f32[10,4,16,128]{3,2,1,0:T(8,128)S(1)}) custom-call(f32[4,16,128]{2,1,0:T(8,128)} %kappa.5, f32[4,16,128]{2,1,0:T(8,128)} %mass.5, f32[8,4,16,128]{3,2,1,0:T(8,128)} %sources.1), custom_call_target="tpu_custom_call" | custom-call | tf_op jit(solution)/shard_map/edges/pallas_call | solution.py:390
  6.7 4.0 %collective-permute-start = (f32[10,3,16,128]{3,2,1,0:T(8,128)S(1)}, f32[10,3,16,128]{3,2,1,0:T(8,128)S(1)}, u32[]{:S(2)}, u32[]{:S(2)}) collective-permute-start(f32[10,3,16,128]{3,2,1,0:T(8,128)S(1)} %get-tuple-element.9), channel_id=1, source_target_pairs={{0,4},{4,8},{8,12},{12,16},{16,20},{20,24},{24,28},{28,32},{32,36}... | collective-permute-start | bytes 737288 | tf_op jit(solution)/shard_map/ppermute | solution.py:398
  10.7 1.9 %collective-permute-start.1 = (f32[10,3,16,128]{3,2,1,0:T(8,128)S(1)}, f32[10,3,16,128]{3,2,1,0:T(8,128)S(1)}, u32[]{:S(2)}, u32[]{:S(2)}) collective-permute-start(f32[10,3,16,128]{3,2,1,0:T(8,128)S(1)} %get-tuple-element.10), channel_id=1, source_target_pairs={{4,0},{8,4},{12,8},{16,12},{20,16},{24,20},{28,24},{32,28},{36,32}... | collective-permute-start | bytes 737288 | tf_op jit(solution)/shard_map/ppermute | solution.py:399
  12.7 0.1 add_convert_fusion.edge
  12.7 1.1 %collective-permute-done.low = f32[10,3,16,128]{3,2,1,0:T(8,128)S(1)} collective-permute-done((f32[10,3,16,128]{3,2,1,0:T(8,128)S(1)}, f32[10,3,16,128]{3,2,1,0:T(8,128)S(1)}, u32[]{:S(2)}, u32[]{:S(2)}) %collective-permute-start) | collective-permute-done | bytes 245792 | tf_op jit(solution)/shard_map/ppermute | solution.py:398
  13.9 4.4 %collective-permute-done.1.high = f32[10,3,16,128]{3,2,1,0:T(8,128)S(1)} collective-permute-done((f32[10,3,16,128]{3,2,1,0:T(8,128)S(1)}, f32[10,3,16,128]{3,2,1,0:T(8,128)S(1)}, u32[]{:S(2)}, u32[]{:S(2)}) %collective-permute-start.1) | collective-permute-done | bytes 245792 | tf_op jit(solution)/shard_map/ppermute | solution.py:399
  18.3 11.8 %sketch_fields.1 = (f32[32,24,128]{2,1,0:T(8,128)}, f32[5760,128]{1,0:T(8,128)}) custom-call(f32[2]{0:T(128)S(1)} %add_convert_fusion.edge, f32[10,3,16,128]{3,2,1,0:T(8,128)S(1)} %collective-permute-done.low, f32[10,3,16,128]{3,2,1,0:T(8,128)S(1)} %collective-permute-done.1.high, f32[10,4,16,128]{3,2,1,0:T(8,128)S(1)} %get-tuple-element.11.own, ...), custom_call_target="tpu_custom_call" | custom-call | flops 96000000 | tf_op jit(solution)/shard_map/sketch_fields/pallas_call | solution.py:407
  30.1 0.0 copy-start.4
  30.2 0.7 copy-done.8
  30.8 0.1 copy-done.9
  30.9 2.1 %load.1 = (f32[64,16,128]{2,1,0:T(8,128)}, f32[64,16,128]{2,1,0:T(8,128)S(1)}) custom-call(f32[5760,128]{1,0:T(8,128)} %get-tuple-element.13._.near_hbm, f32[30,16,128]{2,1,0:T(8,128)} %bitcast.8, f32[30,16,128]{2,1,0:T(8,128)} %bitcast.9, f32[32,16,128]{2,1,0:T(8,128)} %bitcast.13, f32[32,16,128]{2,1,0:T(8,128)} %bitcast.11), custom_call_target="tpu_custom_call" | custom-call | tf_op jit(solution)/shard_map/load/pallas_call | solution.py:436
  33.1 1.7 %collective-permute-start.4 = (f32[64,16,128]{2,1,0:T(8,128)}, f32[64,16,128]{2,1,0:T(8,128)S(1)}, u32[]{:S(2)}, u32[]{:S(2)}) collective-permute-start(f32[64,16,128]{2,1,0:T(8,128)} %get-tuple-element.14), channel_id=1, source_target_pairs={{0,3},{1,0},{2,1},{3,2},{4,7},{5,4},{6,5},{7,6},{8,11},{9,8},{10,9... | collective-permute-start | bytes 1572872 | tf_op jit(solution)/shard_map/ppermute | solution.py:444
  34.8 8.4 %all-to-all-start = ((f32[32,24,128]{2,1,0:T(8,128)}), f32[32,24,128]{2,1,0:T(8,128)S(1)}, u32[]{:S(2)}, u32[]{:S(2)}) async-start(f32[32,24,128]{2,1,0:T(8,128)} %get-tuple-element.12), calls=%async_computation | async-start | bytes 786432 | tf_op jit(solution)/shard_map/all_to_all | solution.py:429
  43.2 0.1 collective-permute-done.4.refs_0_.refs_1_
  43.4 2.9 %collective-permute-start.6 = (f32[24,16,128]{2,1,0:T(8,128)S(1)}, f32[24,16,128]{2,1,0:T(8,128)S(1)}, u32[]{:S(2)}, u32[]{:S(2)}) collective-permute-start(f32[24,16,128]{2,1,0:T(8,128)S(1)} %pad_maximum_fusion), channel_id=1, source_target_pairs={{0,3},{1,0},{2,1},{3,2},{4,7},{5,4},{6,5},{7,6},{8,11},{9,8},{10,9... | collective-permute-start | bytes 589832 | tf_op jit(solution)/shard_map/ppermute | solution.py:450
  46.4 0.3 collective-permute-start.7
  46.6 6.8 %all-to-all-done.pieces = f32[32,24,128]{2,1,0:T(8,128)S(1)} async-done(((f32[32,24,128]{2,1,0:T(8,128)}), f32[32,24,128]{2,1,0:T(8,128)S(1)}, u32[]{:S(2)}, u32[]{:S(2)}) %all-to-all-start) | async-done | bytes 393248 | tf_op jit(solution)/shard_map/all_to_all | solution.py:429
  53.5 1.0 %gram.1 = f32[128,1,128]{2,1,0:T(1,128)} custom-call(f32[32,24,128]{2,1,0:T(8,128)S(1)} %all-to-all-done.pieces), custom_call_target="tpu_custom_call" | custom-call | flops 16000000 | tf_op jit(solution)/shard_map/gram/pallas_call | solution.py:470
  54.5 5.5 %all-to-all-start.1 = ((f32[128,1,128]{2,1,0:T(1,128)}), f32[128,1,128]{2,1,0:T(1,128)S(1)}, u32[]{:S(2)}, u32[]{:S(2)}) async-start(f32[128,1,128]{2,1,0:T(1,128)} %gram.1), calls=%async_computation.1 | async-start | bytes 131072 | tf_op jit(solution)/shard_map/all_to_all | solution.py:478
  60.0 7.0 %shard_map.77.beside_hbm = f32[16,10,64,128]{3,2,1,0:T(8,128)} custom-call(f32[2]{0:T(128)S(1)} %add_convert_fusion.edge, f32[4,16,128]{2,1,0:T(8,128)S(1)} %copy-done.4, f32[4,16,128]{2,1,0:T(8,128)S(1)} %copy-done.5, f32[10,3,16,128]{3,2,1,0:T(8,128)S(1)} %copy-done.1, f32[10,3,16,128]{3,2,1,0:T(8,128)S(1)} %copy-done.3, ...), custom_call_target="tpu_custom_call" | custom-call | flops 38400000 | tf_op jit(solution)/shard_map/pallas_call | solution.py:458
  67.1 3.8 %shard_map.78.beyond_hbm = f32[8,10,64,128]{3,2,1,0:T(8,128)} custom-call(f32[2]{0:T(128)S(1)} %add_convert_fusion.edge, f32[4,16,128]{2,1,0:T(8,128)S(1)} %copy-done.4, f32[4,16,128]{2,1,0:T(8,128)S(1)} %copy-done.5, f32[10,3,16,128]{3,2,1,0:T(8,128)S(1)} %copy-done.1, f32[10,3,16,128]{3,2,1,0:T(8,128)S(1)} %copy-done.3, ...), custom_call_target="tpu_custom_call" | custom-call | flops 19200000 | tf_op jit(solution)/shard_map/pallas_call | solution.py:458
  70.9 8.1 %combine.1 = (f32[4,32,4,16,128]{4,3,2,1,0:T(8,128)}, f32[4,32,4,16,128]{4,3,2,1,0:T(8,128)}) custom-call(s32[1]{0:T(128)} %bitcast.group, f32[64]{0:T(128)S(1)} %copy-done.6, s32[4]{0:T(128)S(1)} %copy-done.7, f32[128,1,128]{2,1,0:T(1,128)S(1)} %all-to-all-done.1.grams, f32[5760,128]{1,0:T(8,128)} %get-tuple-element.13._.near_hbm, ...), custom_call_target="tpu_custom_call" | custom-call | tf_op jit(solution)/shard_map/combine/pallas_call | solution.py:500
  (28 shorter events, 0.1 us)
Async XLA Ops:
  0.6 29.5 %collective-permute-start.3 = (f32[8,4,16,128]{3,2,1,0:T(8,128)}, f32[8,4,16,128]{3,2,1,0:T(8,128)S(1)}, u32[]{:S(2)}, u32[]{:S(2)}) collective-permute-start(f32[8,4,16,128]{3,2,1,0:T(8,128)} %sources.1), channel_id=1, source_target_pairs={{0,1},{1,2},{2,3},{3,0},{4,5},{5,6},{6,7},{7,4},{8,9},{9,10},{10,1... | collective-permute-start | bytes 786440 | tf_op jit(solution)/shard_map/ppermute | solution.py:404
  3.2 27.0 %collective-permute-start.2 = (f32[8,4,16,128]{3,2,1,0:T(8,128)}, f32[8,4,16,128]{3,2,1,0:T(8,128)S(1)}, u32[]{:S(2)}, u32[]{:S(2)}) collective-permute-start(f32[8,4,16,128]{3,2,1,0:T(8,128)} %sources.1), channel_id=1, source_target_pairs={{0,3},{1,0},{2,1},{3,2},{4,7},{5,4},{6,5},{7,6},{8,11},{9,8},{10,9... | collective-permute-start | bytes 786440 | tf_op jit(solution)/shard_map/ppermute | solution.py:403
  6.7 7.2 %collective-permute-start = (f32[10,3,16,128]{3,2,1,0:T(8,128)S(1)}, f32[10,3,16,128]{3,2,1,0:T(8,128)S(1)}, u32[]{:S(2)}, u32[]{:S(2)}) collective-permute-start(f32[10,3,16,128]{3,2,1,0:T(8,128)S(1)} %get-tuple-element.9), channel_id=1, source_target_pairs={{0,4},{4,8},{8,12},{12,16},{16,20},{20,24},{24,28},{28,32},{32,36}... | collective-permute-start | bytes 737288 | tf_op jit(solution)/shard_map/ppermute | solution.py:398
  10.7 7.5 %collective-permute-start.1 = (f32[10,3,16,128]{3,2,1,0:T(8,128)S(1)}, f32[10,3,16,128]{3,2,1,0:T(8,128)S(1)}, u32[]{:S(2)}, u32[]{:S(2)}) collective-permute-start(f32[10,3,16,128]{3,2,1,0:T(8,128)S(1)} %get-tuple-element.10), channel_id=1, source_target_pairs={{4,0},{8,4},{12,8},{16,12},{20,16},{24,20},{28,24},{32,28},{36,32}... | collective-permute-start | bytes 737288 | tf_op jit(solution)/shard_map/ppermute | solution.py:399
  13.9 16.2 %copy-start = (f32[10,3,16,128]{3,2,1,0:T(8,128)}, f32[10,3,16,128]{3,2,1,0:T(8,128)S(1)}, u32[]{:S(2)}) copy-start(f32[10,3,16,128]{3,2,1,0:T(8,128)S(1)} %collective-permute-done.low) | copy-start | bytes 737284
  18.2 11.8 %copy-start.2 = (f32[10,3,16,128]{3,2,1,0:T(8,128)}, f32[10,3,16,128]{3,2,1,0:T(8,128)S(1)}, u32[]{:S(2)}) copy-start(f32[10,3,16,128]{3,2,1,0:T(8,128)S(1)} %collective-permute-done.1.high) | copy-start | bytes 737284
  30.1 29.9 %copy-start.4 = (f32[4,16,128]{2,1,0:T(8,128)S(1)}, f32[4,16,128]{2,1,0:T(8,128)}, u32[]{:S(2)}) copy-start(f32[4,16,128]{2,1,0:T(8,128)} %kappa.5) | copy-start | bytes 98308
  30.1 29.9 %copy-start.5 = (f32[4,16,128]{2,1,0:T(8,128)S(1)}, f32[4,16,128]{2,1,0:T(8,128)}, u32[]{:S(2)}) copy-start(f32[4,16,128]{2,1,0:T(8,128)} %mass.5) | copy-start | bytes 98308
  30.1 0.7 copy-start.8
  30.1 29.9 %copy-start.1 = (f32[10,3,16,128]{3,2,1,0:T(8,128)S(1)}, f32[10,3,16,128]{3,2,1,0:T(8,128)}, u32[]{:S(2)}) copy-start(f32[10,3,16,128]{3,2,1,0:T(8,128)} %copy-done) | copy-start | bytes 737284
  30.1 29.9 %copy-start.3 = (f32[10,3,16,128]{3,2,1,0:T(8,128)S(1)}, f32[10,3,16,128]{3,2,1,0:T(8,128)}, u32[]{:S(2)}) copy-start(f32[10,3,16,128]{3,2,1,0:T(8,128)} %copy-done.2) | copy-start | bytes 737284
  30.2 0.8 copy-start.9
  33.1 10.3 %collective-permute-start.4 = (f32[64,16,128]{2,1,0:T(8,128)}, f32[64,16,128]{2,1,0:T(8,128)S(1)}, u32[]{:S(2)}, u32[]{:S(2)}) collective-permute-start(f32[64,16,128]{2,1,0:T(8,128)} %get-tuple-element.14), channel_id=1, source_target_pairs={{0,3},{1,0},{2,1},{3,2},{4,7},{5,4},{6,5},{7,6},{8,11},{9,8},{10,9... | collective-permute-start | bytes 1572872 | tf_op jit(solution)/shard_map/ppermute | solution.py:444
  34.8 11.5 %collective-permute-start.5 = (f32[64,16,128]{2,1,0:T(8,128)S(1)}, f32[64,16,128]{2,1,0:T(8,128)S(1)}, u32[]{:S(2)}, u32[]{:S(2)}) collective-permute-start(f32[64,16,128]{2,1,0:T(8,128)S(1)} %get-tuple-element.15), channel_id=1, source_target_pairs={{0,1},{1,2},{2,3},{3,0},{4,5},{5,6},{6,7},{7,4},{8,9},{9,10},{10,1... | collective-permute-start | bytes 1572872 | tf_op jit(solution)/shard_map/ppermute | solution.py:445
  34.8 18.7 %all-to-all-start = ((f32[32,24,128]{2,1,0:T(8,128)}), f32[32,24,128]{2,1,0:T(8,128)S(1)}, u32[]{:S(2)}, u32[]{:S(2)}) async-start(f32[32,24,128]{2,1,0:T(8,128)} %get-tuple-element.12), calls=%async_computation | async-start | bytes 786432 | tf_op jit(solution)/shard_map/all_to_all | solution.py:429
  43.4 23.7 %collective-permute-start.6 = (f32[24,16,128]{2,1,0:T(8,128)S(1)}, f32[24,16,128]{2,1,0:T(8,128)S(1)}, u32[]{:S(2)}, u32[]{:S(2)}) collective-permute-start(f32[24,16,128]{2,1,0:T(8,128)S(1)} %pad_maximum_fusion), channel_id=1, source_target_pairs={{0,3},{1,0},{2,1},{3,2},{4,7},{5,4},{6,5},{7,6},{8,11},{9,8},{10,9... | collective-permute-start | bytes 589832 | tf_op jit(solution)/shard_map/ppermute | solution.py:450
  46.4 20.7 %collective-permute-start.7 = (f32[24,16,128]{2,1,0:T(8,128)S(1)}, f32[24,16,128]{2,1,0:T(8,128)S(1)}, u32[]{:S(2)}, u32[]{:S(2)}) collective-permute-start(f32[24,16,128]{2,1,0:T(8,128)S(1)} %pad_maximum_fusion.1), channel_id=1, source_target_pairs={{0,1},{1,2},{2,3},{3,0},{4,5},{5,6},{6,7},{7,4},{8,9},{9,10},{10,1... | collective-permute-start | bytes 589832 | tf_op jit(solution)/shard_map/ppermute | solution.py:451
  54.5 16.4 %all-to-all-start.1 = ((f32[128,1,128]{2,1,0:T(1,128)}), f32[128,1,128]{2,1,0:T(1,128)S(1)}, u32[]{:S(2)}, u32[]{:S(2)}) async-start(f32[128,1,128]{2,1,0:T(1,128)} %gram.1), calls=%async_computation.1 | async-start | bytes 131072 | tf_op jit(solution)/shard_map/all_to_all | solution.py:478
  60.0 10.9 %copy-start.6 = (f32[64]{0:T(128)S(1)}, f32[64]{0:T(128)}, u32[]{:S(2)}) copy-start(f32[64]{0:T(128)} %table.1) | copy-start | bytes 772
  60.0 10.9 %copy-start.7 = (s32[4]{0:T(128)S(1)}, s32[4]{0:T(128)}, u32[]{:S(2)}) copy-start(s32[4]{0:T(128)} %ids.1) | copy-start | bytes 52
where the time goes:
time: 79.4 us; the launch traced here: 79.1 us
  Pallas kernels  35.1 us (44%)
  starting transfers between devices  29.5 us (37%)
  waiting for transfers between devices  12.5 us (16%)
  between operations  1.05 us (1%)
  local copies, waits for them, and re-layouts  0.83 us (1%)
    pallas_call x1, Pallas kernels, on_device(): pl.pallas_call(sketch_kernel, in_specs=[SMEM] + [VMEM] * 3 + [HBM], out_s...  11.8 us
    pallas_call x2, Pallas kernels, far_fields(): pl.pallas_call(functools.partial(far_kernel, parts, outside), in_specs=[S...  10.8 us
    all_to_all x1, starting transfers between devices, on_device(): arrived = lax.all_to_all(pieces, 'dom', 0, 0, tiled=True)  8.41 us
    pallas_call x1, Pallas kernels, on_device(): pl.pallas_call(final_kernel, grid_spec=pltpu.PrefetchScalarGridSpec(num_s...  8.05 us
    all_to_all x1, waiting for transfers between devices, on_device(): arrived = lax.all_to_all(pieces, 'dom', 0, 0, tiled=True)  6.85 us
    all_to_all x1, starting transfers between devices, on_device(): grams = lax.all_to_all(lines, BOTH, 0, 0, tiled=True)  5.47 us
    ppermute x1, waiting for transfers between devices, on_device(): high = lax.ppermute(bottom, 'dom', [(i + 1, i) for i in range(dom - 1)])  4.39 us
    ppermute x1, starting transfers between devices, on_device(): low = lax.ppermute(top, 'dom', [(i, i + 1) for i in range(dom - 1)])  4.05 us
  transfers between devices with their start and end apart: 10, of which 4 were waited for; matrix products, arithmetic and copies ran while one was open for 0% of the time, Pallas kernels for 32%

commit v1 on v0

--- a/solution.py
+++ b/solution.py
@@ -171,43 +171,44 @@
         copy.wait()
 
 
-def far_kernel(parts, outside, edge, kappa, mass, low, high, *refs):
-    planes = list(refs[: len(refs) - 1 - len(outside) - bool(outside)])
-    out, *held = refs[len(planes) :]
-    if outside:
-        *held, sem = held
-        copies = [pltpu.make_async_copy(planes[n], ref, sem.at[i]) for i, (n, ref) in enumerate(zip(outside, held))]
-
-        @pl.when(pl.program_id(0) == 0)
-        def _():
-            for copy in copies:
-                copy.start()
-            for copy in copies:
-                copy.wait()
-
-        for n, ref in zip(outside, held):
-            planes[n] = ref
-    low_on, high_on = edge[0], edge[1]
-    wide_kappa = jnp.concatenate([low[0], kappa[...], high[0]], axis=0)
-    q = jnp.concatenate([low[1], mass[...], high[1]], axis=0) - 1.0
-    slab, ny, nz = kappa.shape
+def wide_coefficients(kappa, mass, low, high):
+    return jnp.concatenate([low[0], kappa, high[0]], axis=0), jnp.concatenate([low[1], mass, high[1]], axis=0) - 1.0
+
+
+def fields_to(out, planes, places, s, wide_kappa, q, low_on, high_on):
+    slab = wide_kappa.shape[0] - 6
+    parts = []
+    for (ref, first), size in zip(places, (3, slab, 3)):
+        parts.append(planes[ref][pl.ds(first + s * size, size)])
+    for f, field in enumerate(ten_fields(jnp.concatenate(parts, axis=0), wide_kappa, q, low_on, high_on)):
+        out[f] = field.reshape(-1, field.shape[2])
+
+
+def far_kernel(sections, edge, kappa, mass, low, high, halo_after, halo_before, after, before, out, *held):
+    *held, sem = held
     here = out.shape[0]
     step = pl.program_id(0)
+    copies = [pltpu.make_async_copy(*pair, sem.at[n]) for n, pair in enumerate(zip((after, before), held))]
+
+    @pl.when(step == 0)
+    def _():
+        for copy in copies:
+            copy.start()
+
+    wide_kappa, q = wide_coefficients(kappa[...], mass[...], low, high)
     base = 0
-    for count, below, middle, above in parts:
+    for (count, *places), copy in zip(sections, copies):
+
+        @pl.when(step == base)
+        def _(copy=copy):
+            copy.wait()
 
         @pl.when((step >= base) & (step < base + count // here))
-        def _(base=base, below=below, middle=middle, above=above):
+        def _(base=base, places=places):
             def one_source(i, carry):
                 s = (step - base) * here + i
-
-                def cut(place, size):
-                    ref, first = place
-                    return planes[ref][pl.ds(first + s * size, size)]
-
-                wide = jnp.concatenate([cut(below, 3), cut(middle, slab), cut(above, 3)], axis=0)
-                for f, field in enumerate(ten_fields(wide, wide_kappa, q, low_on, high_on)):
-                    out[i, f] = field.reshape(slab * ny, nz)
+                planes = (halo_after, held[0], halo_before, held[1])
+                fields_to(out.at[i], planes, places, s, wide_kappa, q, edge[0], edge[1])
                 return carry
 
             lax.fori_loop(0, here, one_source, 0)
@@ -240,7 +241,8 @@
 
 
 def final_kernel(
-    group, table, ids, grams, near_hbm, beside_hbm, beyond_hbm, sol, res, near, far, turned, weights, scalars, sem, arrived
+    sections, group, table, ids, edge, kappa, mass, low, high, third_after, second_after, third_before, second_before,
+    grams, near_hbm, beside_hbm, sol, res, near, far, turned, weights, scalars, sem, arrived,
 ):
     groups = 4
     per_group = grams.shape[0] // (groups * groups)
@@ -253,11 +255,10 @@
     def fetch(n):
         if n == 0:
             return pltpu.make_async_copy(near_hbm, near, arrived.at[0])
-        source, first = (beside_hbm, 0) if n <= beside_steps else (beyond_hbm, beside_steps)
-        taken = source.at[pl.ds((n - 1 - first) * here, here)]
-        return pltpu.make_async_copy(taken, far.at[pl.ds((n - 1) * here, here)], arrived.at[n])
-
-    copies = 1 + far.shape[0] // here
+        rows = pl.ds((n - 1) * here, here)
+        return pltpu.make_async_copy(beside_hbm.at[rows], far.at[rows], arrived.at[n])
+
+    copies = 1 + beside_steps
 
     @pl.when(step == 0)
     def _():
@@ -317,6 +318,17 @@
             weights[8 * n : 8 * (n + 1), :] = value
         copy = pltpu.make_async_copy(weights, scalars, sem)
         copy.start()
+        wide_kappa, q = wide_coefficients(kappa[...], mass[...], low, high)
+        planes = (third_after, second_after, third_before, second_before)
+        base = beside_hbm.shape[0]
+        for count, *places in sections:
+
+            def one_source(s, carry, base=base, places=places):
+                fields_to(far.at[base + s], planes, places, s, wide_kappa, q, edge[0], edge[1])
+                return carry
+
+            lax.fori_loop(0, count, one_source, 0)
+            base = base + count
         copy.wait()
 
     ny = sol.shape[3]
@@ -450,23 +462,6 @@
     third_after = lax.ppermute(third(second_after, 0), "shift", from_next)
     third_before = lax.ppermute(third(second_before, skip), "shift", from_last)
 
-    here = 4
-
-    def far_fields(parts, outside, *planes):
-        count = sum(part[0] for part in parts)
-        shape = (count, FIELDS, slab * ny, nz)
-        return pl.pallas_call(
-            functools.partial(far_kernel, parts, outside),
-            in_specs=[SMEM] + [VMEM] * 4 + [HBM if n in outside else VMEM for n in range(len(planes))],
-            grid=(count // here,),
-            out_specs=pl.BlockSpec((here, *shape[1:]), lambda i: (i, 0, 0, 0)),
-            out_shape=pltpu.HBM(shape, f32),
-            scratch_shapes=[pltpu.VMEM(planes[n].shape, f32) for n in outside]
-            + [pltpu.SemaphoreType.DMA((len(outside),))] * bool(outside),
-            compiler_params=limit(20),
-            cost_estimate=cost(count * 0.3),
-        )(edge, kappa, mass, low, high, *planes)
-
     lines = pl.pallas_call(
         gram_kernel,
         in_specs=[VMEM],
@@ -476,15 +471,26 @@
         name="gram",
     )(pltpu.with_memory_space_constraint(arrived, pltpu.VMEM))
     grams = lax.all_to_all(lines, BOTH, 0, 0, tiled=True)
-    beside = far_fields(
-        ((per_group, (0, 0), (1, 0), (0, ends)), (per_group, (2, 0), (3, 0), (2, ends))),
-        (1, 3),
-        second_after, in_hbm(flat(after)), second_before, in_hbm(flat(before)),
-    )
-    beyond = far_fields(
-        ((half, (0, 0), (1, 2 * ends), (0, skip)), (half, (2, 0), (3, 2 * ends), (2, skip))),
-        (),
-        third_after, second_after, third_before, second_before,
+    far_here = 4
+    far_shape = (2 * per_group, FIELDS, slab * ny, nz)
+    slabs = pltpu.VMEM((per_group * slab, ny, nz), f32)
+    beside = pl.pallas_call(
+        functools.partial(
+            far_kernel,
+            ((per_group, (0, 0), (1, 0), (0, ends)), (per_group, (2, 0), (3, 0), (2, ends))),
+        ),
+        in_specs=[SMEM] + [VMEM] * 6 + [HBM] * 2,
+        grid=(far_shape[0] // far_here,),
+        out_specs=pl.BlockSpec((far_here, *far_shape[1:]), lambda i: (i, 0, 0, 0)),
+        out_shape=pltpu.HBM(far_shape, f32),
+        scratch_shapes=[slabs, slabs, pltpu.SemaphoreType.DMA((2,))],
+        compiler_params=limit(20),
+        cost_estimate=cost(6),
+        name="fields_beside",
+    )(edge, kappa, mass, low, high, second_after, second_before, in_hbm(flat(after)), in_hbm(flat(before)))
+    sections = (
+        (half, (0, 0), (1, 2 * ends), (0, skip)),
+        (half, (2, 0), (3, 2 * ends), (2, skip)),
     )
 
     here = per_group
@@ -498,11 +504,11 @@
     spec = pl.BlockSpec((shifts, here, slab, ny, nz), place)
     shape = jax.ShapeDtypeStruct((shifts, total, slab, ny, nz), f32)
     return pl.pallas_call(
-        final_kernel,
+        functools.partial(final_kernel, sections),
         grid_spec=pltpu.PrefetchScalarGridSpec(
             num_scalar_prefetch=1,
             grid=(steps,),
-            in_specs=[SMEM, SMEM, VMEM, HBM, HBM, HBM],
+            in_specs=[SMEM] * 3 + [VMEM] * 9 + [HBM] * 2,
             out_specs=[spec, spec],
             scratch_shapes=[
                 pltpu.VMEM(near.shape, f32),
@@ -511,13 +517,17 @@
                 pltpu.VMEM((56, 128), f32),
                 pltpu.SMEM((56, 128), f32),
                 pltpu.SemaphoreType.DMA,
-                pltpu.SemaphoreType.DMA((1 + (total - per_group) // here,)),
+                pltpu.SemaphoreType.DMA((1 + far_shape[0] // here,)),
             ],
         ),
         out_shape=[shape, shape],
         compiler_params=limit(36),
         name="combine",
-    )(group, shift_table, shift_ids, grams, in_hbm(near), in_hbm(beside), in_hbm(beyond))
+    )(
+        group, shift_table, shift_ids, edge, kappa, mass, low, high,
+        third_after, second_after, third_before, second_before,
+        grams, in_hbm(near), in_hbm(beside),
+    )
 
 
 def solution(mesh):

time: 79.4 us -> 78.5 us (0.989)
  Pallas kernels: 35.1 us -> 31.5 us
  waiting for transfers between devices: 12.5 us -> 15.1 us
    pallas_call x3 -> x2, Pallas kernels: 18.9 us -> 15.3 us  [the longest x1 8.33 us: on_device(): pl.pallas_call(functools.partial(final_kernel, sections), grid_spec=pltpu...]
    all_to_all x1, waiting for transfers between devices: 0.01 us -> 2.66 us  [on_device(): grams = lax.all_to_all(lines, BOTH, 0, 0, tiled=True)]
  transfers between devices with their start and end apart: 10 -> 10, of which waited for: 4 -> 5; matrix products, arithmetic and copies ran while one was open for 0% -> 0% of each run, Pallas kernels for 32% -> 27%
where the time goes in v1:
time: 78.5 us; the launch traced here: 78.1 us
  Pallas kernels  31.5 us (40%)
  starting transfers between devices  29.5 us (38%)
  waiting for transfers between devices  15.1 us (19%)
  between operations  1.04 us (1%)
  local copies, waits for them, and re-layouts  0.83 us (1%)
    pallas_call x1, Pallas kernels, on_device(): pl.pallas_call(sketch_kernel, in_specs=[SMEM] + [VMEM] * 3 + [HBM], out_s...  11.8 us
    all_to_all x1, starting transfers between devices, on_device(): arrived = lax.all_to_all(pieces, 'dom', 0, 0, tiled=True)  8.41 us
    pallas_call x1, Pallas kernels, on_device(): pl.pallas_call(functools.partial(final_kernel, sections), grid_spec=pltpu...  8.33 us
    pallas_call x1, Pallas kernels, on_device(): pl.pallas_call(functools.partial(far_kernel, ((per_group, (0, 0), (1, 0),...  6.94 us
    all_to_all x1, waiting for transfers between devices, on_device(): arrived = lax.all_to_all(pieces, 'dom', 0, 0, tiled=True)  6.82 us
    all_to_all x1, starting transfers between devices, on_device(): grams = lax.all_to_all(lines, BOTH, 0, 0, tiled=True)  5.49 us
    ppermute x1, waiting for transfers between devices, on_device(): high = lax.ppermute(bottom, 'dom', [(i + 1, i) for i in range(dom - 1)])  4.39 us
    ppermute x1, starting transfers between devices, on_device(): low = lax.ppermute(top, 'dom', [(i, i + 1) for i in range(dom - 1)])  4.05 us
  transfers between devices with their start and end apart: 10, of which 5 were waited for; matrix products, arithmetic and copies ran while one was open for 0% of the time, Pallas kernels for 27%

profile of v1, /device:TPU:1, one launch (start us, length us, event | category | flops | bytes accessed | tf_op | source)
XLA Modules:
  0.0 78.1 jit_solution(1040907528062660803)
XLA Ops:
  0.6 2.5 %collective-permute-start.3 = (f32[8,4,16,128]{3,2,1,0:T(8,128)}, f32[8,4,16,128]{3,2,1,0:T(8,128)S(1)}, u32[]{:S(2)}, u32[]{:S(2)}) collective-permute-start(f32[8,4,16,128]{3,2,1,0:T(8,128)} %sources.1), channel_id=1, source_target_pairs={{0,1},{1,2},{2,3},{3,0},{4,5},{5,6},{6,7},{7,4},{8,9},{9,10},{10,1... | collective-permute-start | bytes 786440 | tf_op jit(solution)/shard_map/ppermute | solution.py:416
  3.2 2.2 %collective-permute-start.2 = (f32[8,4,16,128]{3,2,1,0:T(8,128)}, f32[8,4,16,128]{3,2,1,0:T(8,128)S(1)}, u32[]{:S(2)}, u32[]{:S(2)}) collective-permute-start(f32[8,4,16,128]{3,2,1,0:T(8,128)} %sources.1), channel_id=1, source_target_pairs={{0,3},{1,0},{2,1},{3,2},{4,7},{5,4},{6,5},{7,6},{8,11},{9,8},{10,9... | collective-permute-start | bytes 786440 | tf_op jit(solution)/shard_map/ppermute | solution.py:415
  5.4 1.3 %edges.1 = (f32[10,3,16,128]{3,2,1,0:T(8,128)S(1)}, f32[10,3,16,128]{3,2,1,0:T(8,128)S(1)}, f32[10,4,16,128]{3,2,1,0:T(8,128)S(1)}) custom-call(f32[4,16,128]{2,1,0:T(8,128)} %kappa.5, f32[4,16,128]{2,1,0:T(8,128)} %mass.5, f32[8,4,16,128]{3,2,1,0:T(8,128)} %sources.1), custom_call_target="tpu_custom_call" | custom-call | tf_op jit(solution)/shard_map/edges/pallas_call | solution.py:402
  6.7 4.0 %collective-permute-start = (f32[10,3,16,128]{3,2,1,0:T(8,128)S(1)}, f32[10,3,16,128]{3,2,1,0:T(8,128)S(1)}, u32[]{:S(2)}, u32[]{:S(2)}) collective-permute-start(f32[10,3,16,128]{3,2,1,0:T(8,128)S(1)} %get-tuple-element.9), channel_id=1, source_target_pairs={{0,4},{4,8},{8,12},{12,16},{16,20},{20,24},{24,28},{28,32},{32,36}... | collective-permute-start | bytes 737288 | tf_op jit(solution)/shard_map/ppermute | solution.py:410
  10.7 1.9 %collective-permute-start.1 = (f32[10,3,16,128]{3,2,1,0:T(8,128)S(1)}, f32[10,3,16,128]{3,2,1,0:T(8,128)S(1)}, u32[]{:S(2)}, u32[]{:S(2)}) collective-permute-start(f32[10,3,16,128]{3,2,1,0:T(8,128)S(1)} %get-tuple-element.10), channel_id=1, source_target_pairs={{4,0},{8,4},{12,8},{16,12},{20,16},{24,20},{28,24},{32,28},{36,32}... | collective-permute-start | bytes 737288 | tf_op jit(solution)/shard_map/ppermute | solution.py:411
  12.7 0.1 add_convert_fusion.edge
  12.7 1.1 %collective-permute-done.low = f32[10,3,16,128]{3,2,1,0:T(8,128)S(1)} collective-permute-done((f32[10,3,16,128]{3,2,1,0:T(8,128)S(1)}, f32[10,3,16,128]{3,2,1,0:T(8,128)S(1)}, u32[]{:S(2)}, u32[]{:S(2)}) %collective-permute-start) | collective-permute-done | bytes 245792 | tf_op jit(solution)/shard_map/ppermute | solution.py:410
  13.9 4.4 %collective-permute-done.1.high = f32[10,3,16,128]{3,2,1,0:T(8,128)S(1)} collective-permute-done((f32[10,3,16,128]{3,2,1,0:T(8,128)S(1)}, f32[10,3,16,128]{3,2,1,0:T(8,128)S(1)}, u32[]{:S(2)}, u32[]{:S(2)}) %collective-permute-start.1) | collective-permute-done | bytes 245792 | tf_op jit(solution)/shard_map/ppermute | solution.py:411
  18.3 11.8 %sketch_fields.1 = (f32[32,24,128]{2,1,0:T(8,128)}, f32[5760,128]{1,0:T(8,128)}) custom-call(f32[2]{0:T(128)S(1)} %add_convert_fusion.edge, f32[10,3,16,128]{3,2,1,0:T(8,128)S(1)} %collective-permute-done.low, f32[10,3,16,128]{3,2,1,0:T(8,128)S(1)} %collective-permute-done.1.high, f32[10,4,16,128]{3,2,1,0:T(8,128)S(1)} %get-tuple-element.11.own, ...), custom_call_target="tpu_custom_call" | custom-call | flops 96000000 | tf_op jit(solution)/shard_map/sketch_fields/pallas_call | solution.py:419
  30.1 0.0 copy-start.4
  30.2 0.7 copy-done.8
  30.8 0.1 copy-done.9
  30.9 2.1 %load.1 = (f32[64,16,128]{2,1,0:T(8,128)}, f32[64,16,128]{2,1,0:T(8,128)S(1)}) custom-call(f32[5760,128]{1,0:T(8,128)} %get-tuple-element.12._.near_hbm, f32[30,16,128]{2,1,0:T(8,128)} %bitcast.8, f32[30,16,128]{2,1,0:T(8,128)} %bitcast.9, f32[32,16,128]{2,1,0:T(8,128)} %bitcast.13, f32[32,16,128]{2,1,0:T(8,128)} %bitcast.11), custom_call_target="tpu_custom_call" | custom-call | tf_op jit(solution)/shard_map/load/pallas_call | solution.py:448
  33.1 1.7 %collective-permute-start.4 = (f32[64,16,128]{2,1,0:T(8,128)}, f32[64,16,128]{2,1,0:T(8,128)S(1)}, u32[]{:S(2)}, u32[]{:S(2)}) collective-permute-start(f32[64,16,128]{2,1,0:T(8,128)} %get-tuple-element.13), channel_id=1, source_target_pairs={{0,3},{1,0},{2,1},{3,2},{4,7},{5,4},{6,5},{7,6},{8,11},{9,8},{10,9... | collective-permute-start | bytes 1572872 | tf_op jit(solution)/shard_map/ppermute | solution.py:456
  34.8 8.4 %all-to-all-start = ((f32[32,24,128]{2,1,0:T(8,128)}), f32[32,24,128]{2,1,0:T(8,128)S(1)}, u32[]{:S(2)}, u32[]{:S(2)}) async-start(f32[32,24,128]{2,1,0:T(8,128)} %get-tuple-element.15), calls=%async_computation | async-start | bytes 786432 | tf_op jit(solution)/shard_map/all_to_all | solution.py:441
  43.2 0.1 collective-permute-done.4.halo_after.second_after
  43.4 2.9 %collective-permute-start.5 = (f32[24,16,128]{2,1,0:T(8,128)S(1)}, f32[24,16,128]{2,1,0:T(8,128)S(1)}, u32[]{:S(2)}, u32[]{:S(2)}) collective-permute-start(f32[24,16,128]{2,1,0:T(8,128)S(1)} %pad_maximum_fusion), channel_id=1, source_target_pairs={{0,3},{1,0},{2,1},{3,2},{4,7},{5,4},{6,5},{7,6},{8,11},{9,8},{10,9... | collective-permute-start | bytes 589832 | tf_op jit(solution)/shard_map/ppermute | solution.py:462
  46.4 0.3 collective-permute-start.7
  46.7 6.8 %all-to-all-done.pieces = f32[32,24,128]{2,1,0:T(8,128)S(1)} async-done(((f32[32,24,128]{2,1,0:T(8,128)}), f32[32,24,128]{2,1,0:T(8,128)S(1)}, u32[]{:S(2)}, u32[]{:S(2)}) %all-to-all-start) | async-done | bytes 393248 | tf_op jit(solution)/shard_map/all_to_all | solution.py:441
  53.5 1.0 %gram.1 = f32[128,1,128]{2,1,0:T(1,128)} custom-call(f32[32,24,128]{2,1,0:T(8,128)S(1)} %all-to-all-done.pieces), custom_call_target="tpu_custom_call" | custom-call | flops 16000000 | tf_op jit(solution)/shard_map/gram/pallas_call | solution.py:465
  54.5 5.5 %all-to-all-start.1 = ((f32[128,1,128]{2,1,0:T(1,128)}), f32[128,1,128]{2,1,0:T(1,128)S(1)}, u32[]{:S(2)}, u32[]{:S(2)}) async-start(f32[128,1,128]{2,1,0:T(1,128)} %gram.1), calls=%async_computation.1 | async-start | bytes 131072 | tf_op jit(solution)/shard_map/all_to_all | solution.py:473
  60.0 6.9 %fields_beside.1.beside_hbm = f32[16,10,64,128]{3,2,1,0:T(8,128)} custom-call(f32[2]{0:T(128)S(1)} %add_convert_fusion.edge, f32[4,16,128]{2,1,0:T(8,128)S(1)} %copy-done.4, f32[4,16,128]{2,1,0:T(8,128)S(1)} %copy-done.5, f32[10,3,16,128]{3,2,1,0:T(8,128)S(1)} %copy-done.1, f32[10,3,16,128]{3,2,1,0:T(8,128)S(1)} %copy-done.3, ...), custom_call_target="tpu_custom_call" | custom-call | flops 48000000 | tf_op jit(solution)/shard_map/fields_beside/pallas_call | solution.py:477
  67.0 2.7 %all-to-all-done.1.grams = f32[128,1,128]{2,1,0:T(1,128)S(1)} async-done(((f32[128,1,128]{2,1,0:T(1,128)}), f32[128,1,128]{2,1,0:T(1,128)S(1)}, u32[]{:S(2)}, u32[]{:S(2)}) %all-to-all-start.1) | async-done | bytes 65568 | tf_op jit(solution)/shard_map/all_to_all | solution.py:473
  69.7 8.3 %combine.1 = (f32[4,32,4,16,128]{4,3,2,1,0:T(8,128)}, f32[4,32,4,16,128]{4,3,2,1,0:T(8,128)}) custom-call(s32[1]{0:T(128)} %bitcast.group, f32[64]{0:T(128)S(1)} %copy-done.6, s32[4]{0:T(128)S(1)} %copy-done.7, f32[2]{0:T(128)S(1)} %add_convert_fusion.edge, f32[4,16,128]{2,1,0:T(8,128)S(1)} %copy-done.4, f32[4,16,128]{2,1,0:T(8,128)S(1)} %copy-done.5, ...), custom_call_target="tpu_custom_call" | custom-call | tf_op jit(solution)/shard_map/combine/pallas_call | solution.py:506
  (27 shorter events, 0.1 us)
Async XLA Ops:
  0.6 29.5 %collective-permute-start.3 = (f32[8,4,16,128]{3,2,1,0:T(8,128)}, f32[8,4,16,128]{3,2,1,0:T(8,128)S(1)}, u32[]{:S(2)}, u32[]{:S(2)}) collective-permute-start(f32[8,4,16,128]{3,2,1,0:T(8,128)} %sources.1), channel_id=1, source_target_pairs={{0,1},{1,2},{2,3},{3,0},{4,5},{5,6},{6,7},{7,4},{8,9},{9,10},{10,1... | collective-permute-start | bytes 786440 | tf_op jit(solution)/shard_map/ppermute | solution.py:416
  3.2 27.0 %collective-permute-start.2 = (f32[8,4,16,128]{3,2,1,0:T(8,128)}, f32[8,4,16,128]{3,2,1,0:T(8,128)S(1)}, u32[]{:S(2)}, u32[]{:S(2)}) collective-permute-start(f32[8,4,16,128]{3,2,1,0:T(8,128)} %sources.1), channel_id=1, source_target_pairs={{0,3},{1,0},{2,1},{3,2},{4,7},{5,4},{6,5},{7,6},{8,11},{9,8},{10,9... | collective-permute-start | bytes 786440 | tf_op jit(solution)/shard_map/ppermute | solution.py:415
  6.7 7.2 %collective-permute-start = (f32[10,3,16,128]{3,2,1,0:T(8,128)S(1)}, f32[10,3,16,128]{3,2,1,0:T(8,128)S(1)}, u32[]{:S(2)}, u32[]{:S(2)}) collective-permute-start(f32[10,3,16,128]{3,2,1,0:T(8,128)S(1)} %get-tuple-element.9), channel_id=1, source_target_pairs={{0,4},{4,8},{8,12},{12,16},{16,20},{20,24},{24,28},{28,32},{32,36}... | collective-permute-start | bytes 737288 | tf_op jit(solution)/shard_map/ppermute | solution.py:410
  10.7 7.5 %collective-permute-start.1 = (f32[10,3,16,128]{3,2,1,0:T(8,128)S(1)}, f32[10,3,16,128]{3,2,1,0:T(8,128)S(1)}, u32[]{:S(2)}, u32[]{:S(2)}) collective-permute-start(f32[10,3,16,128]{3,2,1,0:T(8,128)S(1)} %get-tuple-element.10), channel_id=1, source_target_pairs={{4,0},{8,4},{12,8},{16,12},{20,16},{24,20},{28,24},{32,28},{36,32}... | collective-permute-start | bytes 737288 | tf_op jit(solution)/shard_map/ppermute | solution.py:411
  13.9 16.2 %copy-start = (f32[10,3,16,128]{3,2,1,0:T(8,128)}, f32[10,3,16,128]{3,2,1,0:T(8,128)S(1)}, u32[]{:S(2)}) copy-start(f32[10,3,16,128]{3,2,1,0:T(8,128)S(1)} %collective-permute-done.low) | copy-start | bytes 737284
  18.2 11.8 %copy-start.2 = (f32[10,3,16,128]{3,2,1,0:T(8,128)}, f32[10,3,16,128]{3,2,1,0:T(8,128)S(1)}, u32[]{:S(2)}) copy-start(f32[10,3,16,128]{3,2,1,0:T(8,128)S(1)} %collective-permute-done.1.high) | copy-start | bytes 737284
  30.1 29.9 %copy-start.4 = (f32[4,16,128]{2,1,0:T(8,128)S(1)}, f32[4,16,128]{2,1,0:T(8,128)}, u32[]{:S(2)}) copy-start(f32[4,16,128]{2,1,0:T(8,128)} %kappa.5) | copy-start | bytes 98308
  30.1 29.9 %copy-start.5 = (f32[4,16,128]{2,1,0:T(8,128)S(1)}, f32[4,16,128]{2,1,0:T(8,128)}, u32[]{:S(2)}) copy-start(f32[4,16,128]{2,1,0:T(8,128)} %mass.5) | copy-start | bytes 98308
  30.1 0.7 copy-start.8
  30.1 29.9 %copy-start.1 = (f32[10,3,16,128]{3,2,1,0:T(8,128)S(1)}, f32[10,3,16,128]{3,2,1,0:T(8,128)}, u32[]{:S(2)}) copy-start(f32[10,3,16,128]{3,2,1,0:T(8,128)} %copy-done) | copy-start | bytes 737284
  30.1 29.9 %copy-start.3 = (f32[10,3,16,128]{3,2,1,0:T(8,128)S(1)}, f32[10,3,16,128]{3,2,1,0:T(8,128)}, u32[]{:S(2)}) copy-start(f32[10,3,16,128]{3,2,1,0:T(8,128)} %copy-done.2) | copy-start | bytes 737284
  30.2 0.8 copy-start.9
  33.1 10.3 %collective-permute-start.4 = (f32[64,16,128]{2,1,0:T(8,128)}, f32[64,16,128]{2,1,0:T(8,128)S(1)}, u32[]{:S(2)}, u32[]{:S(2)}) collective-permute-start(f32[64,16,128]{2,1,0:T(8,128)} %get-tuple-element.13), channel_id=1, source_target_pairs={{0,3},{1,0},{2,1},{3,2},{4,7},{5,4},{6,5},{7,6},{8,11},{9,8},{10,9... | collective-permute-start | bytes 1572872 | tf_op jit(solution)/shard_map/ppermute | solution.py:456
  34.8 11.5 %collective-permute-start.6 = (f32[64,16,128]{2,1,0:T(8,128)S(1)}, f32[64,16,128]{2,1,0:T(8,128)S(1)}, u32[]{:S(2)}, u32[]{:S(2)}) collective-permute-start(f32[64,16,128]{2,1,0:T(8,128)S(1)} %get-tuple-element.14), channel_id=1, source_target_pairs={{0,1},{1,2},{2,3},{3,0},{4,5},{5,6},{6,7},{7,4},{8,9},{9,10},{10,1... | collective-permute-start | bytes 1572872 | tf_op jit(solution)/shard_map/ppermute | solution.py:457
  34.8 18.7 %all-to-all-start = ((f32[32,24,128]{2,1,0:T(8,128)}), f32[32,24,128]{2,1,0:T(8,128)S(1)}, u32[]{:S(2)}, u32[]{:S(2)}) async-start(f32[32,24,128]{2,1,0:T(8,128)} %get-tuple-element.15), calls=%async_computation | async-start | bytes 786432 | tf_op jit(solution)/shard_map/all_to_all | solution.py:441
  43.4 26.2 %collective-permute-start.5 = (f32[24,16,128]{2,1,0:T(8,128)S(1)}, f32[24,16,128]{2,1,0:T(8,128)S(1)}, u32[]{:S(2)}, u32[]{:S(2)}) collective-permute-start(f32[24,16,128]{2,1,0:T(8,128)S(1)} %pad_maximum_fusion), channel_id=1, source_target_pairs={{0,3},{1,0},{2,1},{3,2},{4,7},{5,4},{6,5},{7,6},{8,11},{9,8},{10,9... | collective-permute-start | bytes 589832 | tf_op jit(solution)/shard_map/ppermute | solution.py:462
  46.4 23.3 %copy-start.6 = (f32[64]{0:T(128)S(1)}, f32[64]{0:T(128)}, u32[]{:S(2)}) copy-start(f32[64]{0:T(128)} %table.1) | copy-start | bytes 772
  46.4 23.3 %copy-start.7 = (s32[4]{0:T(128)S(1)}, s32[4]{0:T(128)}, u32[]{:S(2)}) copy-start(s32[4]{0:T(128)} %ids.1) | copy-start | bytes 52
  46.4 23.2 %collective-permute-start.7 = (f32[24,16,128]{2,1,0:T(8,128)S(1)}, f32[24,16,128]{2,1,0:T(8,128)S(1)}, u32[]{:S(2)}, u32[]{:S(2)}) collective-permute-start(f32[24,16,128]{2,1,0:T(8,128)S(1)} %pad_maximum_fusion.1), channel_id=1, source_target_pairs={{0,1},{1,2},{2,3},{3,0},{4,5},{5,6},{6,7},{7,4},{8,9},{9,10},{10,1... | collective-permute-start | bytes 589832 | tf_op jit(solution)/shard_map/ppermute | solution.py:463
  54.5 15.1 %all-to-all-start.1 = ((f32[128,1,128]{2,1,0:T(1,128)}), f32[128,1,128]{2,1,0:T(1,128)S(1)}, u32[]{:S(2)}, u32[]{:S(2)}) async-start(f32[128,1,128]{2,1,0:T(1,128)} %gram.1), calls=%async_computation.1 | async-start | bytes 131072 | tf_op jit(solution)/shard_map/all_to_all | solution.py:473

commit v2 on v1

--- a/solution.py
+++ b/solution.py
@@ -22,12 +22,11 @@
 
 def around(field):
     inner = field[1:-1]
-    rows = lax.broadcasted_iota(jnp.int32, inner.shape, 1)
     lanes = lax.broadcasted_iota(jnp.int32, inner.shape, 2)
-    ny, nz = inner.shape[1], inner.shape[2]
+    nz = inner.shape[2]
     total = field[2:] + field[:-2]
-    total = total + jnp.where(rows == 0, 0.0, pltpu.roll(inner, 1, 1))
-    total = total + jnp.where(rows == ny - 1, 0.0, pltpu.roll(inner, ny - 1, 1))
+    edge = jnp.zeros((inner.shape[0], 1, nz), jnp.float32)
+    total = total + jnp.concatenate([edge, inner[:, :-1]], axis=1) + jnp.concatenate([inner[:, 1:], edge], axis=1)
     total = total + jnp.where(lanes == 0, 0.0, pltpu.roll(inner, 1, 2))
     return total + jnp.where(lanes == nz - 1, 0.0, pltpu.roll(inner, nz - 1, 2))
 

time: 78.5 us -> 78.5 us (level)
  no operation moved by 1% of the time
where the time goes in v2:
time: 78.5 us; the launch traced here: 78.1 us
  Pallas kernels  31.5 us (40%)
  starting transfers between devices  29.5 us (38%)
  waiting for transfers between devices  15.2 us (19%)
  between operations  1.04 us (1%)
  local copies, waits for them, and re-layouts  0.83 us (1%)
    pallas_call x1, Pallas kernels, on_device(): pl.pallas_call(sketch_kernel, in_specs=[SMEM] + [VMEM] * 3 + [HBM], out_s...  11.8 us
    all_to_all x1, starting transfers between devices, on_device(): arrived = lax.all_to_all(pieces, 'dom', 0, 0, tiled=True)  8.41 us
    pallas_call x1, Pallas kernels, on_device(): pl.pallas_call(functools.partial(final_kernel, sections), grid_spec=pltpu...  8.31 us
    pallas_call x1, Pallas kernels, on_device(): pl.pallas_call(functools.partial(far_kernel, ((per_group, (0, 0), (1, 0),...  6.89 us
    all_to_all x1, waiting for transfers between devices, on_device(): arrived = lax.all_to_all(pieces, 'dom', 0, 0, tiled=True)  6.82 us
    all_to_all x1, starting transfers between devices, on_device(): grams = lax.all_to_all(lines, BOTH, 0, 0, tiled=True)  5.49 us
    ppermute x1, waiting for transfers between devices, on_device(): high = lax.ppermute(bottom, 'dom', [(i + 1, i) for i in range(dom - 1)])  4.39 us
    ppermute x1, starting transfers between devices, on_device(): low = lax.ppermute(top, 'dom', [(i, i + 1) for i in range(dom - 1)])  4.05 us
  transfers between devices with their start and end apart: 10, of which 5 were waited for; matrix products, arithmetic and copies ran while one was open for 0% of the time, Pallas kernels for 27%

profile of v2, /device:TPU:1, one launch (start us, length us, event | category | flops | bytes accessed | tf_op | source)
XLA Modules:
  0.0 78.1 jit_solution(13446601509383101658)
XLA Ops:
  0.6 2.5 %collective-permute-start.3 = (f32[8,4,16,128]{3,2,1,0:T(8,128)}, f32[8,4,16,128]{3,2,1,0:T(8,128)S(1)}, u32[]{:S(2)}, u32[]{:S(2)}) collective-permute-start(f32[8,4,16,128]{3,2,1,0:T(8,128)} %sources.1), channel_id=1, source_target_pairs={{0,1},{1,2},{2,3},{3,0},{4,5},{5,6},{6,7},{7,4},{8,9},{9,10},{10,1... | collective-permute-start | bytes 786440 | tf_op jit(solution)/shard_map/ppermute | solution.py:415
  3.2 2.2 %collective-permute-start.2 = (f32[8,4,16,128]{3,2,1,0:T(8,128)}, f32[8,4,16,128]{3,2,1,0:T(8,128)S(1)}, u32[]{:S(2)}, u32[]{:S(2)}) collective-permute-start(f32[8,4,16,128]{3,2,1,0:T(8,128)} %sources.1), channel_id=1, source_target_pairs={{0,3},{1,0},{2,1},{3,2},{4,7},{5,4},{6,5},{7,6},{8,11},{9,8},{10,9... | collective-permute-start | bytes 786440 | tf_op jit(solution)/shard_map/ppermute | solution.py:414
  5.4 1.3 %edges.1 = (f32[10,3,16,128]{3,2,1,0:T(8,128)S(1)}, f32[10,3,16,128]{3,2,1,0:T(8,128)S(1)}, f32[10,4,16,128]{3,2,1,0:T(8,128)S(1)}) custom-call(f32[4,16,128]{2,1,0:T(8,128)} %kappa.5, f32[4,16,128]{2,1,0:T(8,128)} %mass.5, f32[8,4,16,128]{3,2,1,0:T(8,128)} %sources.1), custom_call_target="tpu_custom_call" | custom-call | tf_op jit(solution)/shard_map/edges/pallas_call | solution.py:401
  6.7 4.0 %collective-permute-start = (f32[10,3,16,128]{3,2,1,0:T(8,128)S(1)}, f32[10,3,16,128]{3,2,1,0:T(8,128)S(1)}, u32[]{:S(2)}, u32[]{:S(2)}) collective-permute-start(f32[10,3,16,128]{3,2,1,0:T(8,128)S(1)} %get-tuple-element.9), channel_id=1, source_target_pairs={{0,4},{4,8},{8,12},{12,16},{16,20},{20,24},{24,28},{28,32},{32,36}... | collective-permute-start | bytes 737288 | tf_op jit(solution)/shard_map/ppermute | solution.py:409
  10.7 1.9 %collective-permute-start.1 = (f32[10,3,16,128]{3,2,1,0:T(8,128)S(1)}, f32[10,3,16,128]{3,2,1,0:T(8,128)S(1)}, u32[]{:S(2)}, u32[]{:S(2)}) collective-permute-start(f32[10,3,16,128]{3,2,1,0:T(8,128)S(1)} %get-tuple-element.10), channel_id=1, source_target_pairs={{4,0},{8,4},{12,8},{16,12},{20,16},{24,20},{28,24},{32,28},{36,32}... | collective-permute-start | bytes 737288 | tf_op jit(solution)/shard_map/ppermute | solution.py:410
  12.7 0.1 add_convert_fusion.edge
  12.7 1.1 %collective-permute-done.low = f32[10,3,16,128]{3,2,1,0:T(8,128)S(1)} collective-permute-done((f32[10,3,16,128]{3,2,1,0:T(8,128)S(1)}, f32[10,3,16,128]{3,2,1,0:T(8,128)S(1)}, u32[]{:S(2)}, u32[]{:S(2)}) %collective-permute-start) | collective-permute-done | bytes 245792 | tf_op jit(solution)/shard_map/ppermute | solution.py:409
  13.9 4.4 %collective-permute-done.1.high = f32[10,3,16,128]{3,2,1,0:T(8,128)S(1)} collective-permute-done((f32[10,3,16,128]{3,2,1,0:T(8,128)S(1)}, f32[10,3,16,128]{3,2,1,0:T(8,128)S(1)}, u32[]{:S(2)}, u32[]{:S(2)}) %collective-permute-start.1) | collective-permute-done | bytes 245792 | tf_op jit(solution)/shard_map/ppermute | solution.py:410
  18.3 11.8 %sketch_fields.1 = (f32[32,24,128]{2,1,0:T(8,128)}, f32[5760,128]{1,0:T(8,128)}) custom-call(f32[2]{0:T(128)S(1)} %add_convert_fusion.edge, f32[10,3,16,128]{3,2,1,0:T(8,128)S(1)} %collective-permute-done.low, f32[10,3,16,128]{3,2,1,0:T(8,128)S(1)} %collective-permute-done.1.high, f32[10,4,16,128]{3,2,1,0:T(8,128)S(1)} %get-tuple-element.11.own, ...), custom_call_target="tpu_custom_call" | custom-call | flops 96000000 | tf_op jit(solution)/shard_map/sketch_fields/pallas_call | solution.py:418
  30.1 0.0 copy-start.4
  30.2 0.7 copy-done.8
  30.8 0.1 copy-done.9
  30.9 2.1 %load.1 = (f32[64,16,128]{2,1,0:T(8,128)}, f32[64,16,128]{2,1,0:T(8,128)S(1)}) custom-call(f32[5760,128]{1,0:T(8,128)} %get-tuple-element.12._.near_hbm, f32[30,16,128]{2,1,0:T(8,128)} %bitcast.8, f32[30,16,128]{2,1,0:T(8,128)} %bitcast.9, f32[32,16,128]{2,1,0:T(8,128)} %bitcast.13, f32[32,16,128]{2,1,0:T(8,128)} %bitcast.11), custom_call_target="tpu_custom_call" | custom-call | tf_op jit(solution)/shard_map/load/pallas_call | solution.py:447
  33.1 1.7 %collective-permute-start.4 = (f32[64,16,128]{2,1,0:T(8,128)}, f32[64,16,128]{2,1,0:T(8,128)S(1)}, u32[]{:S(2)}, u32[]{:S(2)}) collective-permute-start(f32[64,16,128]{2,1,0:T(8,128)} %get-tuple-element.13), channel_id=1, source_target_pairs={{0,3},{1,0},{2,1},{3,2},{4,7},{5,4},{6,5},{7,6},{8,11},{9,8},{10,9... | collective-permute-start | bytes 1572872 | tf_op jit(solution)/shard_map/ppermute | solution.py:455
  34.8 8.4 %all-to-all-start = ((f32[32,24,128]{2,1,0:T(8,128)}), f32[32,24,128]{2,1,0:T(8,128)S(1)}, u32[]{:S(2)}, u32[]{:S(2)}) async-start(f32[32,24,128]{2,1,0:T(8,128)} %get-tuple-element.15), calls=%async_computation | async-start | bytes 786432 | tf_op jit(solution)/shard_map/all_to_all | solution.py:440
  43.2 0.1 collective-permute-done.4.halo_after.second_after
  43.4 2.9 %collective-permute-start.5 = (f32[24,16,128]{2,1,0:T(8,128)S(1)}, f32[24,16,128]{2,1,0:T(8,128)S(1)}, u32[]{:S(2)}, u32[]{:S(2)}) collective-permute-start(f32[24,16,128]{2,1,0:T(8,128)S(1)} %pad_maximum_fusion), channel_id=1, source_target_pairs={{0,3},{1,0},{2,1},{3,2},{4,7},{5,4},{6,5},{7,6},{8,11},{9,8},{10,9... | collective-permute-start | bytes 589832 | tf_op jit(solution)/shard_map/ppermute | solution.py:461
  46.4 0.3 collective-permute-start.7
  46.7 6.8 %all-to-all-done.pieces = f32[32,24,128]{2,1,0:T(8,128)S(1)} async-done(((f32[32,24,128]{2,1,0:T(8,128)}), f32[32,24,128]{2,1,0:T(8,128)S(1)}, u32[]{:S(2)}, u32[]{:S(2)}) %all-to-all-start) | async-done | bytes 393248 | tf_op jit(solution)/shard_map/all_to_all | solution.py:440
  53.5 1.0 %gram.1 = f32[128,1,128]{2,1,0:T(1,128)} custom-call(f32[32,24,128]{2,1,0:T(8,128)S(1)} %all-to-all-done.pieces), custom_call_target="tpu_custom_call" | custom-call | flops 16000000 | tf_op jit(solution)/shard_map/gram/pallas_call | solution.py:464
  54.5 5.5 %all-to-all-start.1 = ((f32[128,1,128]{2,1,0:T(1,128)}), f32[128,1,128]{2,1,0:T(1,128)S(1)}, u32[]{:S(2)}, u32[]{:S(2)}) async-start(f32[128,1,128]{2,1,0:T(1,128)} %gram.1), calls=%async_computation.1 | async-start | bytes 131072 | tf_op jit(solution)/shard_map/all_to_all | solution.py:472
  60.0 6.9 %fields_beside.1.beside_hbm = f32[16,10,64,128]{3,2,1,0:T(8,128)} custom-call(f32[2]{0:T(128)S(1)} %add_convert_fusion.edge, f32[4,16,128]{2,1,0:T(8,128)S(1)} %copy-done.4, f32[4,16,128]{2,1,0:T(8,128)S(1)} %copy-done.5, f32[10,3,16,128]{3,2,1,0:T(8,128)S(1)} %copy-done.1, f32[10,3,16,128]{3,2,1,0:T(8,128)S(1)} %copy-done.3, ...), custom_call_target="tpu_custom_call" | custom-call | flops 48000000 | tf_op jit(solution)/shard_map/fields_beside/pallas_call | solution.py:476
  66.9 2.7 %all-to-all-done.1.grams = f32[128,1,128]{2,1,0:T(1,128)S(1)} async-done(((f32[128,1,128]{2,1,0:T(1,128)}), f32[128,1,128]{2,1,0:T(1,128)S(1)}, u32[]{:S(2)}, u32[]{:S(2)}) %all-to-all-start.1) | async-done | bytes 65568 | tf_op jit(solution)/shard_map/all_to_all | solution.py:472
  69.7 8.3 %combine.1 = (f32[4,32,4,16,128]{4,3,2,1,0:T(8,128)}, f32[4,32,4,16,128]{4,3,2,1,0:T(8,128)}) custom-call(s32[1]{0:T(128)} %bitcast.group, f32[64]{0:T(128)S(1)} %copy-done.6, s32[4]{0:T(128)S(1)} %copy-done.7, f32[2]{0:T(128)S(1)} %add_convert_fusion.edge, f32[4,16,128]{2,1,0:T(8,128)S(1)} %copy-done.4, f32[4,16,128]{2,1,0:T(8,128)S(1)} %copy-done.5, ...), custom_call_target="tpu_custom_call" | custom-call | tf_op jit(solution)/shard_map/combine/pallas_call | solution.py:505
  (27 shorter events, 0.1 us)
Async XLA Ops:
  0.6 29.5 %collective-permute-start.3 = (f32[8,4,16,128]{3,2,1,0:T(8,128)}, f32[8,4,16,128]{3,2,1,0:T(8,128)S(1)}, u32[]{:S(2)}, u32[]{:S(2)}) collective-permute-start(f32[8,4,16,128]{3,2,1,0:T(8,128)} %sources.1), channel_id=1, source_target_pairs={{0,1},{1,2},{2,3},{3,0},{4,5},{5,6},{6,7},{7,4},{8,9},{9,10},{10,1... | collective-permute-start | bytes 786440 | tf_op jit(solution)/shard_map/ppermute | solution.py:415
  3.2 27.0 %collective-permute-start.2 = (f32[8,4,16,128]{3,2,1,0:T(8,128)}, f32[8,4,16,128]{3,2,1,0:T(8,128)S(1)}, u32[]{:S(2)}, u32[]{:S(2)}) collective-permute-start(f32[8,4,16,128]{3,2,1,0:T(8,128)} %sources.1), channel_id=1, source_target_pairs={{0,3},{1,0},{2,1},{3,2},{4,7},{5,4},{6,5},{7,6},{8,11},{9,8},{10,9... | collective-permute-start | bytes 786440 | tf_op jit(solution)/shard_map/ppermute | solution.py:414
  6.7 7.2 %collective-permute-start = (f32[10,3,16,128]{3,2,1,0:T(8,128)S(1)}, f32[10,3,16,128]{3,2,1,0:T(8,128)S(1)}, u32[]{:S(2)}, u32[]{:S(2)}) collective-permute-start(f32[10,3,16,128]{3,2,1,0:T(8,128)S(1)} %get-tuple-element.9), channel_id=1, source_target_pairs={{0,4},{4,8},{8,12},{12,16},{16,20},{20,24},{24,28},{28,32},{32,36}... | collective-permute-start | bytes 737288 | tf_op jit(solution)/shard_map/ppermute | solution.py:409
  10.7 7.5 %collective-permute-start.1 = (f32[10,3,16,128]{3,2,1,0:T(8,128)S(1)}, f32[10,3,16,128]{3,2,1,0:T(8,128)S(1)}, u32[]{:S(2)}, u32[]{:S(2)}) collective-permute-start(f32[10,3,16,128]{3,2,1,0:T(8,128)S(1)} %get-tuple-element.10), channel_id=1, source_target_pairs={{4,0},{8,4},{12,8},{16,12},{20,16},{24,20},{28,24},{32,28},{36,32}... | collective-permute-start | bytes 737288 | tf_op jit(solution)/shard_map/ppermute | solution.py:410
  13.9 16.2 %copy-start = (f32[10,3,16,128]{3,2,1,0:T(8,128)}, f32[10,3,16,128]{3,2,1,0:T(8,128)S(1)}, u32[]{:S(2)}) copy-start(f32[10,3,16,128]{3,2,1,0:T(8,128)S(1)} %collective-permute-done.low) | copy-start | bytes 737284
  18.2 11.8 %copy-start.2 = (f32[10,3,16,128]{3,2,1,0:T(8,128)}, f32[10,3,16,128]{3,2,1,0:T(8,128)S(1)}, u32[]{:S(2)}) copy-start(f32[10,3,16,128]{3,2,1,0:T(8,128)S(1)} %collective-permute-done.1.high) | copy-start | bytes 737284
  30.1 29.9 %copy-start.4 = (f32[4,16,128]{2,1,0:T(8,128)S(1)}, f32[4,16,128]{2,1,0:T(8,128)}, u32[]{:S(2)}) copy-start(f32[4,16,128]{2,1,0:T(8,128)} %kappa.5) | copy-start | bytes 98308
  30.1 29.9 %copy-start.5 = (f32[4,16,128]{2,1,0:T(8,128)S(1)}, f32[4,16,128]{2,1,0:T(8,128)}, u32[]{:S(2)}) copy-start(f32[4,16,128]{2,1,0:T(8,128)} %mass.5) | copy-start | bytes 98308
  30.1 0.7 copy-start.8
  30.1 29.9 %copy-start.1 = (f32[10,3,16,128]{3,2,1,0:T(8,128)S(1)}, f32[10,3,16,128]{3,2,1,0:T(8,128)}, u32[]{:S(2)}) copy-start(f32[10,3,16,128]{3,2,1,0:T(8,128)} %copy-done) | copy-start | bytes 737284
  30.1 29.9 %copy-start.3 = (f32[10,3,16,128]{3,2,1,0:T(8,128)S(1)}, f32[10,3,16,128]{3,2,1,0:T(8,128)}, u32[]{:S(2)}) copy-start(f32[10,3,16,128]{3,2,1,0:T(8,128)} %copy-done.2) | copy-start | bytes 737284
  30.2 0.8 copy-start.9
  33.1 10.3 %collective-permute-start.4 = (f32[64,16,128]{2,1,0:T(8,128)}, f32[64,16,128]{2,1,0:T(8,128)S(1)}, u32[]{:S(2)}, u32[]{:S(2)}) collective-permute-start(f32[64,16,128]{2,1,0:T(8,128)} %get-tuple-element.13), channel_id=1, source_target_pairs={{0,3},{1,0},{2,1},{3,2},{4,7},{5,4},{6,5},{7,6},{8,11},{9,8},{10,9... | collective-permute-start | bytes 1572872 | tf_op jit(solution)/shard_map/ppermute | solution.py:455
  34.8 11.5 %collective-permute-start.6 = (f32[64,16,128]{2,1,0:T(8,128)S(1)}, f32[64,16,128]{2,1,0:T(8,128)S(1)}, u32[]{:S(2)}, u32[]{:S(2)}) collective-permute-start(f32[64,16,128]{2,1,0:T(8,128)S(1)} %get-tuple-element.14), channel_id=1, source_target_pairs={{0,1},{1,2},{2,3},{3,0},{4,5},{5,6},{6,7},{7,4},{8,9},{9,10},{10,1... | collective-permute-start | bytes 1572872 | tf_op jit(solution)/shard_map/ppermute | solution.py:456
  34.8 18.7 %all-to-all-start = ((f32[32,24,128]{2,1,0:T(8,128)}), f32[32,24,128]{2,1,0:T(8,128)S(1)}, u32[]{:S(2)}, u32[]{:S(2)}) async-start(f32[32,24,128]{2,1,0:T(8,128)} %get-tuple-element.15), calls=%async_computation | async-start | bytes 786432 | tf_op jit(solution)/shard_map/all_to_all | solution.py:440
  43.4 26.2 %collective-permute-start.5 = (f32[24,16,128]{2,1,0:T(8,128)S(1)}, f32[24,16,128]{2,1,0:T(8,128)S(1)}, u32[]{:S(2)}, u32[]{:S(2)}) collective-permute-start(f32[24,16,128]{2,1,0:T(8,128)S(1)} %pad_maximum_fusion), channel_id=1, source_target_pairs={{0,3},{1,0},{2,1},{3,2},{4,7},{5,4},{6,5},{7,6},{8,11},{9,8},{10,9... | collective-permute-start | bytes 589832 | tf_op jit(solution)/shard_map/ppermute | solution.py:461
  46.4 23.3 %copy-start.6 = (f32[64]{0:T(128)S(1)}, f32[64]{0:T(128)}, u32[]{:S(2)}) copy-start(f32[64]{0:T(128)} %table.1) | copy-start | bytes 772
  46.4 23.3 %copy-start.7 = (s32[4]{0:T(128)S(1)}, s32[4]{0:T(128)}, u32[]{:S(2)}) copy-start(s32[4]{0:T(128)} %ids.1) | copy-start | bytes 52
  46.4 23.2 %collective-permute-start.7 = (f32[24,16,128]{2,1,0:T(8,128)S(1)}, f32[24,16,128]{2,1,0:T(8,128)S(1)}, u32[]{:S(2)}, u32[]{:S(2)}) collective-permute-start(f32[24,16,128]{2,1,0:T(8,128)S(1)} %pad_maximum_fusion.1), channel_id=1, source_target_pairs={{0,1},{1,2},{2,3},{3,0},{4,5},{5,6},{6,7},{7,4},{8,9},{9,10},{10,1... | collective-permute-start | bytes 589832 | tf_op jit(solution)/shard_map/ppermute | solution.py:462
  54.5 15.1 %all-to-all-start.1 = ((f32[128,1,128]{2,1,0:T(1,128)}), f32[128,1,128]{2,1,0:T(1,128)S(1)}, u32[]{:S(2)}, u32[]{:S(2)}) async-start(f32[128,1,128]{2,1,0:T(1,128)} %gram.1), calls=%async_computation.1 | async-start | bytes 131072 | tf_op jit(solution)/shard_map/all_to_all | solution.py:472
